TPU v7x, 32 devices: a whole 2x2x4 slice. The times are simulated.
32 devices in a mesh: gx: 4 (over y, core), gy: 4 (over z), gz: 2 (over x).
Axes of the slice: x: 2, y: 2, z: 4, core: 2. Of those that a mesh axis runs over, the one named last changes fastest.
Arguments:
- tokens: bfloat16 [256, 7168], P(('gx', 'gy', 'gz')), may hold values from -6 to 6
- expert_ids: int32 [256, 8], P(('gx', 'gy', 'gz')), may hold values from 0 to 15, as said below
- slot_ids: int32 [256, 8], P(('gx', 'gy', 'gz')), may hold values from 0 to 7, as said below
- route_weight: bfloat16 [256, 8], P(('gx', 'gy', 'gz')), may hold values from 0.099609375 to 0.59765625
- gate_weight: bfloat16 [16, 7168, 2048], P(('gx', 'gy'), None, 'gz'), may hold values from -0.0625 to 0.0625
- up_weight: bfloat16 [16, 7168, 2048], P(('gx', 'gy'), None, 'gz'), may hold values from -0.0625 to 0.0625
- down_weight: bfloat16 [16, 2048, 7168], P(('gx', 'gy'), 'gz'), may hold values from -0.125 to 0.125
- expert_bias: float32 [16], replicated, may hold values from -3 to 3
Outputs:
- combined: bfloat16 [256, 7168], P(('gx', 'gy', 'gz'))
- expert_load: int32 [16], replicated
- new_bias: float32 [16], replicated
Inputs may be any that keep to these rules, and one draw needn't show every extreme that they name: `expert_ids`: the 8 experts of a token are different. Among the 8 tokens of one device no expert is named more than 8 times; one expert is named by every token of every device. `slot_ids`: for each device and expert, the routes of that device's tokens to that expert hold different slots.
All inputs are finite; a program needn't handle non-finite values.
Results may differ from a plain program's by a relative error of at most 0.015.
Values may be sent and summed in bfloat16 or wider, within the bound.
A program may use at most 128 MiB of HBM per device.

v0:
```python
import jax
import jax.numpy as jnp
from jax import lax
from jax.sharding import PartitionSpec as P

PLACE_LIMIT = 8
bias_rate = 0.001


def pack_rows(targets, tokens, row_total):
    selection = jnp.any(
        targets[None, :, :] == jnp.arange(row_total, dtype=jnp.int32)[:, None, None], axis=2
    )
    return jnp.dot(
        selection.astype(jnp.bfloat16), tokens, preferred_element_type=jnp.float32
    ).astype(jnp.bfloat16)


def send_rows(buffer):
    arrived = lax.all_to_all(buffer, ("gx", "gy", "gz"), split_axis=1, concat_axis=1, tiled=True)
    return arrived


def return_rows(buffer):
    arrived = lax.all_to_all(buffer, ("gx", "gy", "gz"), split_axis=1, concat_axis=1, tiled=True)
    return arrived


def body(
    tokens, expert_ids, slot_ids, route_weight, gate_weight, up_weight, down_weight, expert_bias
):
    experts = lax.axis_size("gx") * lax.axis_size("gy")
    gz_parts = lax.axis_size("gz")
    devices = experts * gz_parts
    tok_rows, model_width = tokens.shape
    route_count = expert_ids.shape[1]
    capacity = PLACE_LIMIT
    slot_share = capacity // gz_parts
    expert_index = jnp.arange(experts, dtype=jnp.int32)
    local_hits = jnp.sum((expert_ids[:, :, None] == expert_index).astype(jnp.int32), axis=(0, 1))
    expert_load = lax.psum(local_hits, ("gx", "gy", "gz"))
    mean_load = tok_rows * devices * route_count // experts
    new_bias = expert_bias + bias_rate * jnp.sign((mean_load - expert_load).astype(jnp.float32))
    back_rows = slot_ids % slot_share * devices + expert_ids * gz_parts + slot_ids // slot_share
    packed = pack_rows(slot_ids * experts + expert_ids, tokens, capacity * experts)
    repeated = jnp.broadcast_to(
        packed.reshape(capacity, experts, 1, model_width),
        (capacity, experts, gz_parts, model_width),
    )
    received = send_rows(repeated.reshape(capacity, devices, model_width))
    gate_mat = gate_weight[0]
    up_mat = up_weight[0]
    down_mat = down_weight[0]
    flat_rows = received.reshape(slot_share * lax.axis_size("gz") * devices, model_width)
    gate_act = jnp.dot(flat_rows, gate_mat, preferred_element_type=jnp.float32)
    up_act = jnp.dot(flat_rows, up_mat, preferred_element_type=jnp.float32)
    hidden = (jax.nn.silu(gate_act) * up_act).astype(jnp.bfloat16)
    partial_out = jnp.dot(hidden, down_mat, preferred_element_type=jnp.float32)
    summed = lax.psum_scatter(
        partial_out.reshape(slot_share * lax.axis_size("gz"), devices, model_width).astype(
            jnp.bfloat16
        ),
        "gz",
        scatter_dimension=0,
        tiled=True,
    )
    answers = return_rows(summed)
    flat_answers = answers.reshape(slot_share * devices, model_width)
    spread = jnp.where(
        back_rows[:, :, None] == jnp.arange(slot_share * devices, dtype=jnp.int32),
        route_weight.astype(jnp.float32)[:, :, None],
        0.0,
    )
    mixing = jnp.sum(spread, axis=1).astype(jnp.bfloat16)
    combined = jnp.dot(mixing, flat_answers, preferred_element_type=jnp.float32).astype(
        jnp.bfloat16
    )
    return (combined, expert_load, new_bias)


def solution(mesh):
    return jax.shard_map(
        body,
        mesh=mesh,
        in_specs=(
            P(("gx", "gy", "gz"), None),
            P(("gx", "gy", "gz"), None),
            P(("gx", "gy", "gz"), None),
            P(("gx", "gy", "gz"), None),
            P(("gx", "gy"), None, "gz"),
            P(("gx", "gy"), None, "gz"),
            P(("gx", "gy"), "gz", None),
            P(),
        ),
        out_specs=(P(("gx", "gy", "gz"), None), P(), P()),
        check_vma=False,
    )
```

profile of v0, /device:TPU:0, one launch (start us, length us, event | category | flops | bytes accessed | tf_op | source)
XLA Modules:
  0.0 253.8 jit_solution(9949804390127732930)
XLA Ops:
  7.2 0.0 copy-start
  7.2 0.0 reduce-scatter.2.cloned.1.call-start
  7.2 0.7 fusion.18
  7.9 0.1 fusion.15
  8.0 0.0 copy-done
  8.1 0.7 convolution_convert_fusion
  8.8 1.0 copy.17
  9.8 0.4 broadcast_in_dim.29
  10.2 0.0 copy-start.4
  10.2 90.8 %all_to_all.10 = bf16[8,32,7168]{2,0,1:T(8,128)(2,1)S(1)} all-to-all(bf16[8,32,7168]{2,0,1:T(8,128)(2,1)S(1)} %bitcast.28), channel_id=1, replica_groups=mesh['gx'=4,'gy'=4,'gz'=2] {'gx','gy','gz'}, dimensions={1} | all-to-all | bytes 7340032 | tf_op jit(solution)/shard_map/all_to_all | solution.py:20
  101.0 2.0 copy.18
  103.0 4.1 %fusion.4 = f32[256,1024]{1,0:T(8,128)S(1)} fusion(bf16[256,7168]{1,0:T(8,128)(2,1)S(1)} %bitcast.31, bf16[1,7168,1024]{2,1,0:T(8,128)(2,1)S(1)} %copy-done.4), kind=kOutput, calls=%fused_computation.4 | convolution fusion | flops 3758096384 | bytes 19398656 | tf_op jit(solution)/shard_map/dot_general | solution.py:55
  107.1 7.6 %fusion.12 = bf16[256,1024]{1,0:T(8,128)(2,1)S(1)} fusion(bf16[256,7168]{1,0:T(8,128)(2,1)S(1)} %bitcast.32, bf16[1,7168,1024]{2,1,0:T(8,128)(2,1)} %param.13, f32[256,1024]{1,0:T(8,128)S(1)} %fusion.4), kind=kOutput, calls=%fused_computation.10 | convolution fusion | flops 3759669248 | bytes 19922944 | tf_op jit(solution)/shard_map/dot_general | solution.py:56
  114.7 10.6 %fusion.6 = bf16[8,32,7168]{2,1,0:T(8,128)(2,1)} fusion(bf16[8,32,1024]{2,1,0:T(8,128)(2,1)S(1)} %bitcast.33, bf16[1,1024,7168]{2,1,0:T(8,128)(2,1)} %param.14), kind=kOutput, calls=%fused_computation.6 | convolution fusion | flops 3759931392 | bytes 18874368 | tf_op jit(solution)/shard_map/dot_general | solution.py:58
  125.3 0.0 reduce-scatter.2.cloned.1.call-update
  125.3 0.0 copy-start.2
  125.4 0.0 copy-start.3
  125.4 0.0 copy-start.5
  125.4 47.0 %reduce-scatter.2.cloned.1.call-done = bf16[4,32,7168]{2,1,0:T(8,128)(2,1)} async-done(((bf16[8,32,7168]{2,1,0:T(8,128)(2,1)}), bf16[4,32,7168]{2,1,0:T(8,128)(2,1)}) %reduce-scatter.2.cloned.1.call-update) | async-done | bytes 1835024 | tf_op jit(solution)/shard_map/reduce_scatter | solution.py:59
  172.4 4.2 %copy.19 = bf16[4,32,7168]{2,0,1:T(4,128)(2,1)} copy(bf16[4,32,7168]{2,1,0:T(8,128)(2,1)} %reduce-scatter.2.cloned.1.call-done) | data formatting | bytes 3670016 | tf_op jit(solution)/shard_map/reduce_scatter | solution.py:59
  176.6 4.6 %all-to-all-start.1 = ((bf16[4,32,7168]{2,0,1:T(4,128)(2,1)}), bf16[4,32,7168]{2,0,1:T(4,128)(2,1)S(1)}, u32[]{:S(2)}, u32[]{:S(2)}) async-start(bf16[4,32,7168]{2,0,1:T(4,128)(2,1)} %copy.19), calls=%async_computation.2 | async-start | bytes 3670016 | tf_op jit(solution)/shard_map/all_to_all | solution.py:25
  181.2 0.0 copy-done.2
  181.2 0.0 copy-start.1
  181.2 0.1 convert_reduce_fusion
  181.3 63.4 %psum.7 = s32[16]{0:T(128)S(1)} all-reduce(s32[16]{0:T(128)S(1)} %convert_reduce_fusion), channel_id=1, replica_groups=mesh['gx'=4,'gy'=4,'gz'=2] {'gx','gy','gz'}, use_global_device_ids=true, to_apply=%region_4.5 | all-reduce | flops 16 | bytes 128 | tf_op jit(solution)/shard_map/psum | solution.py:41
  244.7 0.1 select_reduce_fusion
  244.8 0.0 copy-done.5
  244.8 0.5 multiply_add_fusion.1
  245.4 0.0 all-to-all-done.1
  245.4 0.5 copy.20
  245.9 1.0 convolution_convert_fusion.1
  246.9 0.0 copy-done.1
  (5 shorter events, 0.0 us)
Async XLA Ops:
  7.2 0.9 copy-start
  7.2 165.2 %reduce-scatter.2.cloned.1.call-start = ((), (), s32[]{:S(2)}) async-start(), calls=%async_computation.3 | async-start | bytes 5505024 | tf_op jit(solution)/shard_map/reduce_scatter | solution.py:59
  10.2 92.8 %copy-start.4 = (bf16[1,7168,1024]{2,1,0:T(8,128)(2,1)S(1)}, bf16[1,7168,1024]{2,1,0:T(8,128)(2,1)}, u32[]{:S(2)}) copy-start(bf16[1,7168,1024]{2,1,0:T(8,128)(2,1)} %param.12) | copy-start | bytes 44040196
  125.3 55.9 %copy-start.2 = (s32[8,8]{1,0:T(8,128)S(1)}, s32[8,8]{1,0:T(8,128)}, u32[]{:S(2)}) copy-start(s32[8,8]{1,0:T(8,128)} %param.9) | copy-start | bytes 772
  125.4 119.4 %copy-start.3 = (bf16[8,8]{1,0:T(8,128)(2,1)S(1)}, bf16[8,8]{1,0:T(8,128)(2,1)}, u32[]{:S(2)}) copy-start(bf16[8,8]{1,0:T(8,128)(2,1)} %param.11) | copy-start | bytes 388
  125.4 119.5 %copy-start.5 = (f32[16]{0:T(128)S(1)}, f32[16]{0:T(128)}, u32[]{:S(2)}) copy-start(f32[16]{0:T(128)} %param.15) | copy-start | bytes 196
  176.6 68.8 %all-to-all-start.1 = ((bf16[4,32,7168]{2,0,1:T(4,128)(2,1)}), bf16[4,32,7168]{2,0,1:T(4,128)(2,1)S(1)}, u32[]{:S(2)}, u32[]{:S(2)}) async-start(bf16[4,32,7168]{2,0,1:T(4,128)(2,1)} %copy.19), calls=%async_computation.2 | async-start | bytes 3670016 | tf_op jit(solution)/shard_map/all_to_all | solution.py:25
  181.2 65.7 %copy-start.1 = (bf16[8,7168]{1,0:T(8,128)(2,1)S(1)}, bf16[8,7168]{1,0:T(8,128)(2,1)}, u32[]{:S(2)}) copy-start(bf16[8,7168]{1,0:T(8,128)(2,1)} %param.8) | copy-start | bytes 344068
  244.7 2.2 copy-start.6
Sparse Core Ops, SparseCore 0:
  125.5 46.9 reduce-scatter.1
where the time goes:
time: 254 us
  blocking collectives  154 us (61%)
  waiting for transfers between devices  47.1 us (19%)
  matrix products  24 us (9%)
  between operations  14.2 us (6%)
  local copies, waits for them, and re-layouts  8.22 us (3%)
  starting transfers between devices  4.65 us (2%)
    all_to_all x1, blocking collectives, send_rows(): lax.all_to_all(buffer, ('gx', 'gy', 'gz'), split_axis=1, concat_axis=1, t...  90.8 us
    psum x1, blocking collectives, body(): expert_load = lax.psum(local_hits, ('gx', 'gy', 'gz'))  63.4 us
    reduce_scatter x1, waiting for transfers between devices, body(): lax.psum_scatter(partial_out.reshape(slot_share * lax.axis_size('gz'), de...  47 us
    dot_general x1, matrix products, body(): partial_out = jnp.dot(hidden, down_mat, preferred_element_type=jnp.float32)  10.6 us
    dot_general x1, matrix products, body(): up_act = jnp.dot(flat_rows, up_mat, preferred_element_type=jnp.float32)  7.61 us
  transfers between devices with their start and end apart: 2, of which 1 were waited for; matrix products, arithmetic and copies ran while one was open for 0% of the time, Pallas kernels for 0%

commit v1 on v0

--- a/solution.py
+++ b/solution.py
@@ -17,7 +17,16 @@
 
 
 def send_rows(buffer):
-    arrived = lax.all_to_all(buffer, ("gx", "gy", "gz"), split_axis=1, concat_axis=1, tiled=True)
+    read_the_axis_part = lambda d0, inputs, in_dim: jnp.concatenate(
+        jax.lax.all_to_all(
+            jnp.stack(jnp.split(inputs, jax.lax.axis_size(("gx", "gy", "gz")), axis=d0), axis=0),
+            ("gx", "gy", "gz"),
+            0,
+            0,
+        ),
+        axis=in_dim,
+    )
+    arrived = read_the_axis_part(1, buffer, 1)
     return arrived
 
 

time: 254 us -> 250 us (0.984)
  matrix products: 24 us -> 19 us
    dot_general x1, matrix products: 10.6 us -> 5.53 us  [body(): partial_out = jnp.dot(hidden, down_mat, preferred_element_type=jnp.float32)]
where the time goes in v1:
time: 250 us
  blocking collectives  154 us (62%)
  waiting for transfers between devices  47.1 us (19%)
  matrix products  19 us (8%)
  between operations  14.5 us (6%)
  local copies, waits for them, and re-layouts  8.65 us (3%)
  starting transfers between devices  4.65 us (2%)
    all_to_all x1, blocking collectives, send_rows(): jax.lax.all_to_all(jnp.stack(jnp.split(inputs, jax.lax.axis_size(('gx', '...  90.8 us
    psum x1, blocking collectives, body(): expert_load = lax.psum(local_hits, ('gx', 'gy', 'gz'))  63.4 us
    reduce_scatter x1, waiting for transfers between devices, body(): lax.psum_scatter(partial_out.reshape(slot_share * lax.axis_size('gz'), de...  47 us
    dot_general x1, matrix products, body(): up_act = jnp.dot(flat_rows, up_mat, preferred_element_type=jnp.float32)  7.78 us
    dot_general x1, matrix products, body(): partial_out = jnp.dot(hidden, down_mat, preferred_element_type=jnp.float32)  5.53 us
  transfers between devices with their start and end apart: 2, of which 1 were waited for; matrix products, arithmetic and copies ran while one was open for 0% of the time, Pallas kernels for 0%

profile of v1, /device:TPU:0, one launch (start us, length us, event | category | flops | bytes accessed | tf_op | source)
XLA Modules:
  0.0 249.6 jit_solution(11695127239687724095)
XLA Ops:
  7.2 0.0 copy-start
  7.2 0.0 reduce-scatter.2.cloned.1.call-start
  7.2 0.7 fusion.50
  7.9 0.1 fusion.47
  8.0 0.0 copy-done
  8.1 0.7 convolution_convert_fusion
  8.8 0.0 slice-start
  8.8 1.0 copy.51
  9.8 0.0 slice-start.1
  9.8 0.5 broadcast_in_dim.29
  10.8 0.0 slice-start.2
  10.9 0.0 slice-start.3
  10.9 90.8 %all_to_all.10 = bf16[32,8,1,7168]{3,1,2,0:T(8,128)(2,1)S(1)} all-to-all(bf16[32,8,1,7168]{3,1,2,0:T(8,128)(2,1)S(1)} %fusion.15), channel_id=1, replica_groups=mesh['gx'=4,'gy'=4,'gz'=2] {'gx','gy','gz'}, dimensions={0} | all-to-all | bytes 7340032 | tf_op jit(solution)/shard_map/all_to_all | solution.py:21
  101.6 2.0 copy.52
  103.7 0.0 slice-start.4
  103.7 4.0 %fusion.4 = f32[256,1024]{1,0:T(8,128)S(1)} fusion(bf16[256,7168]{1,0:T(8,128)(2,1)S(1)} %bitcast.192, bf16[1,7168,1024]{2,1,0:T(8,128)(2,1)S(1)} %bitcast.195), kind=kOutput, calls=%fused_computation.4 | convolution fusion | flops 3758096384 | bytes 19398656 | tf_op jit(solution)/shard_map/dot_general | solution.py:64
  107.8 0.0 slice-start.6
  107.8 7.8 %fusion.12 = bf16[256,1024]{1,0:T(8,128)(2,1)S(1)} fusion(bf16[256,7168]{1,0:T(8,128)(2,1)S(1)} %bitcast.193, bf16[1,7168,1024]{2,1,0:T(8,128)(2,1)} %param.13, f32[256,1024]{1,0:T(8,128)S(1)} %fusion.4), kind=kOutput, calls=%fused_computation.10 | convolution fusion | flops 3759669248 | bytes 19922944 | tf_op jit(solution)/shard_map/dot_general | solution.py:65
  115.6 5.5 %fusion.6 = bf16[8,32,7168]{2,1,0:T(8,128)(2,1)} fusion(bf16[8,32,1024]{2,1,0:T(8,128)(2,1)S(1)} %bitcast.198, bf16[1,1024,7168]{2,1,0:T(8,128)(2,1)S(1)} %bitcast.197), kind=kOutput, calls=%fused_computation.6 | convolution fusion | flops 3759931392 | bytes 18874368 | tf_op jit(solution)/shard_map/dot_general | solution.py:67
  121.2 0.0 reduce-scatter.2.cloned.1.call-update
  121.2 0.0 copy-start.2
  121.2 0.0 copy-start.3
  121.2 0.0 copy-start.4
  121.2 47.0 %reduce-scatter.2.cloned.1.call-done = bf16[4,32,7168]{2,1,0:T(8,128)(2,1)} async-done(((bf16[8,32,7168]{2,1,0:T(8,128)(2,1)}), bf16[4,32,7168]{2,1,0:T(8,128)(2,1)}) %reduce-scatter.2.cloned.1.call-update) | async-done | bytes 1835024 | tf_op jit(solution)/shard_map/reduce_scatter | solution.py:68
  168.3 4.2 %copy.53 = bf16[4,32,7168]{2,0,1:T(4,128)(2,1)} copy(bf16[4,32,7168]{2,1,0:T(8,128)(2,1)} %reduce-scatter.2.cloned.1.call-done) | data formatting | bytes 3670016 | tf_op jit(solution)/shard_map/reduce_scatter | solution.py:68
  172.5 4.6 %all-to-all-start.1 = ((bf16[4,32,7168]{2,0,1:T(4,128)(2,1)}), bf16[4,32,7168]{2,0,1:T(4,128)(2,1)S(1)}, u32[]{:S(2)}, u32[]{:S(2)}) async-start(bf16[4,32,7168]{2,0,1:T(4,128)(2,1)} %copy.53), calls=%async_computation.2 | async-start | bytes 3670016 | tf_op jit(solution)/shard_map/all_to_all | solution.py:34
  177.1 0.1 convert_reduce_fusion
  177.2 63.4 %psum.7 = s32[16]{0:T(128)S(1)} all-reduce(s32[16]{0:T(128)S(1)} %convert_reduce_fusion), channel_id=1, replica_groups=mesh['gx'=4,'gy'=4,'gz'=2] {'gx','gy','gz'}, use_global_device_ids=true, to_apply=%region_4.5 | all-reduce | flops 16 | bytes 128 | tf_op jit(solution)/shard_map/psum | solution.py:50
  240.6 0.1 select_reduce_fusion
  240.7 0.5 multiply_add_fusion.1
  241.2 0.5 copy.54
  241.8 1.0 convolution_convert_fusion.1
  (53 shorter events, 0.4 us)
Async XLA Ops:
  7.2 0.9 copy-start
  7.2 161.1 %reduce-scatter.2.cloned.1.call-start = ((), (), s32[]{:S(2)}) async-start(), calls=%async_computation.3 | async-start | bytes 5505024 | tf_op jit(solution)/shard_map/reduce_scatter | solution.py:68
  8.8 94.9 %slice-start = ((s8[14680064]{0:T(1024)(128)(4,1)}), s8[4194304]{0:T(1024)(128)(4,1)S(1)}, s32[]{:S(2)}) async-start(s8[14680064]{0:T(1024)(128)(4,1)} %bitcast.194), calls=%async_computation.4 | async-start | bytes 8388608
  9.8 93.9 %slice-start.1 = ((s8[14680064]{0:T(1024)(128)(4,1)}), s8[4194304]{0:T(1024)(128)(4,1)S(1)}, s32[]{:S(2)}) async-start(s8[14680064]{0:T(1024)(128)(4,1)} %bitcast.194), calls=%async_computation.5 | async-start | bytes 8388608
  10.8 92.9 %slice-start.2 = ((s8[14680064]{0:T(1024)(128)(4,1)}), s8[4194304]{0:T(1024)(128)(4,1)S(1)}, s32[]{:S(2)}) async-start(s8[14680064]{0:T(1024)(128)(4,1)} %bitcast.194), calls=%async_computation.6 | async-start | bytes 8388608
  10.9 92.8 %slice-start.3 = ((s8[14680064]{0:T(1024)(128)(4,1)}), s8[2097152]{0:T(1024)(128)(4,1)S(1)}, s32[]{:S(2)}) async-start(s8[14680064]{0:T(1024)(128)(4,1)} %bitcast.194), calls=%async_computation.7 | async-start | bytes 4194304
  103.7 11.9 %slice-start.4 = ((s8[14680064]{0:T(1024)(128)(4,1)}), s8[2097152]{0:T(1024)(128)(4,1)S(1)}, s32[]{:S(2)}) async-start(s8[14680064]{0:T(1024)(128)(4,1)} %bitcast.196), calls=%async_computation.8 | async-start | bytes 4194304
  103.7 11.9 %slice-start.5 = ((s8[14680064]{0:T(1024)(128)(4,1)}), s8[4194304]{0:T(1024)(128)(4,1)S(1)}, s32[]{:S(2)}) async-start(s8[14680064]{0:T(1024)(128)(4,1)} %bitcast.196), calls=%async_computation.9 | async-start | bytes 8388608
  107.8 7.8 %slice-start.6 = ((s8[14680064]{0:T(1024)(128)(4,1)}), s8[4194304]{0:T(1024)(128)(4,1)S(1)}, s32[]{:S(2)}) async-start(s8[14680064]{0:T(1024)(128)(4,1)} %bitcast.196), calls=%async_computation.10 | async-start | bytes 8388608
  107.8 7.8 %slice-start.7 = ((s8[14680064]{0:T(1024)(128)(4,1)}), s8[4194304]{0:T(1024)(128)(4,1)S(1)}, s32[]{:S(2)}) async-start(s8[14680064]{0:T(1024)(128)(4,1)} %bitcast.196), calls=%async_computation.11 | async-start | bytes 8388608
  121.2 55.9 %copy-start.2 = (s32[8,8]{1,0:T(8,128)S(1)}, s32[8,8]{1,0:T(8,128)}, u32[]{:S(2)}) copy-start(s32[8,8]{1,0:T(8,128)} %param.9) | copy-start | bytes 772
  121.2 119.4 %copy-start.3 = (bf16[8,8]{1,0:T(8,128)(2,1)S(1)}, bf16[8,8]{1,0:T(8,128)(2,1)}, u32[]{:S(2)}) copy-start(bf16[8,8]{1,0:T(8,128)(2,1)} %param.11) | copy-start | bytes 388
  121.2 119.5 %copy-start.4 = (f32[16]{0:T(128)S(1)}, f32[16]{0:T(128)}, u32[]{:S(2)}) copy-start(f32[16]{0:T(128)} %param.15) | copy-start | bytes 196
  172.5 68.8 %all-to-all-start.1 = ((bf16[4,32,7168]{2,0,1:T(4,128)(2,1)}), bf16[4,32,7168]{2,0,1:T(4,128)(2,1)S(1)}, u32[]{:S(2)}, u32[]{:S(2)}) async-start(bf16[4,32,7168]{2,0,1:T(4,128)(2,1)} %copy.53), calls=%async_computation.2 | async-start | bytes 3670016 | tf_op jit(solution)/shard_map/all_to_all | solution.py:34
  177.1 65.7 %copy-start.1 = (bf16[8,7168]{1,0:T(8,128)(2,1)S(1)}, bf16[8,7168]{1,0:T(8,128)(2,1)}, u32[]{:S(2)}) copy-start(bf16[8,7168]{1,0:T(8,128)(2,1)} %param.8) | copy-start | bytes 344068
  240.6 2.2 copy-start.5
Sparse Core Ops, SparseCore 0:
  121.3 46.9 reduce-scatter.1
